TPU v7x, 32 devices: a whole 2x2x4 slice. The times are simulated.
32 devices in a mesh: row: 2 (over core), col: 16 (over z, y, x).
Axes of the slice: x: 2, y: 2, z: 4, core: 2. Of those that a mesh axis runs over, the one named last changes fastest.
Arguments:
- features: bfloat16 [8192, 256], P(('row', 'col')), may hold values from -6 to 6
- layer_weight: bfloat16 [256, 256], replicated, may hold values from -0.375 to 0.375
- layer_bias: float32 [256], replicated, may hold values from -3 to 3
- cotangent: bfloat16 [8192, 256], P(('row', 'col')), may hold values from -6 to 6
- tile_values: bfloat16 [1024, 256, 256], P(('row', 'col')), may hold values from -0.0625 to 0.0625
- tile_index: int32 [1024, 2], P(('row', 'col')), may hold values from -1 to 31, as said below
Outputs:
- activations: bfloat16 [8192, 256], P(('row', 'col'))
- node_grad: bfloat16 [8192, 256], P(('row', 'col'))
- weight_grad: float32 [256, 256], P(('row', 'col'))
- bias_grad: float32 [256], P(('row', 'col'))
Inputs may be any that keep to these rules, and one draw needn't show every extreme that they name: `tile_index`: each pair is (I, J) with I <= J; device r * 16 + c holds only pairs whose I lies in blocks r * 16 * 1 to (r + 1) * 16 - 1 and whose J // 1 equals c modulo 16. Each pair is held by at most one slot among all devices. A device's live slots come first, its empty slots hold -1 in both entries; counts differ from device to device, and some device fills all 32 slots.
All inputs are finite; a program needn't handle non-finite values.
Results may differ from a plain program's by a relative error of at most 0.025.
Values may be sent and summed in bfloat16 or wider, within the bound.
A program may use at most 128 MiB of HBM per device.

v0:
```python
import jax
import jax.numpy as jnp
from jax import lax
from jax.sharding import PartitionSpec as P

BLK_DEV = 1


def aggregate(node_data, tile_values, tile_index):
    tile_size = tile_values.shape[1]
    feature_count = node_data.shape[1]
    column_devices = lax.axis_size("col")
    row_index = lax.axis_index("row")
    column_group = lax.all_gather(node_data, "row", axis=0, tiled=True)
    row_group = lax.all_gather(node_data, "col", axis=0, tiled=True)
    column_blocks = column_group.reshape(-1, tile_size, feature_count)
    row_blocks = row_group.reshape(-1, tile_size, feature_count)
    row_span = row_blocks.shape[0]
    column_span = column_blocks.shape[0]
    block_row = tile_index[:, 0]
    block_column = tile_index[:, 1]
    occupied = block_row >= 0
    row_slot = jnp.where(occupied, block_row - row_index * row_span, 0)
    column_slot = jnp.where(
        occupied, block_column // BLK_DEV // column_devices * BLK_DEV + block_column % BLK_DEV, 0
    )
    column_inputs = jnp.take(column_blocks, column_slot, axis=0)
    row_inputs = jnp.take(row_blocks, row_slot, axis=0)
    forward_terms = jnp.einsum(
        "tnm,tmf->tnf", tile_values, column_inputs, preferred_element_type=jnp.float32
    )
    mirror_terms = jnp.einsum(
        "tmn,tmf->tnf", tile_values, row_inputs, preferred_element_type=jnp.float32
    )
    live = occupied.astype(jnp.float32)[:, None, None]
    row_partial = (
        jnp.zeros((row_span, tile_size, feature_count), jnp.float32)
        .at[row_slot]
        .add(forward_terms * live)
    )
    column_partial = (
        jnp.zeros((column_span, tile_size, feature_count), jnp.float32)
        .at[column_slot]
        .add(mirror_terms * live)
    )
    row_partial = row_partial.reshape(row_span * tile_size, feature_count)
    column_partial = column_partial.reshape(column_span * tile_size, feature_count)
    row_sums = lax.psum_scatter(
        row_partial.astype(jnp.bfloat16), "col", scatter_dimension=0, tiled=True
    ).astype(jnp.float32)
    column_sums = lax.psum_scatter(
        column_partial.astype(jnp.bfloat16), "row", scatter_dimension=0, tiled=True
    ).astype(jnp.float32)
    return (row_sums + column_sums).astype(jnp.bfloat16)


def local(features, layer_weight, layer_bias, cotangent, tile_values, tile_index):
    aggregated = aggregate(features, tile_values, tile_index)
    hidden = jnp.dot(aggregated, layer_weight, preferred_element_type=jnp.float32) + layer_bias
    logistic = jax.nn.sigmoid(hidden)
    activations = (hidden * logistic).astype(jnp.bfloat16)
    derivative = logistic * (1.0 + hidden * (1.0 - logistic))
    hidden_grad = (cotangent.astype(jnp.float32) * derivative).astype(jnp.bfloat16)
    message_grad = jnp.dot(hidden_grad, layer_weight.T, preferred_element_type=jnp.float32).astype(
        jnp.bfloat16
    )
    total_nodes = features.shape[0] * lax.axis_size("row") * lax.axis_size("col")
    grad_scale = total_nodes ** (-0.5)
    weight_part = (
        lax.dot_general(
            aggregated, hidden_grad, (((0,), (0,)), ((), ())), preferred_element_type=jnp.float32
        )
        * grad_scale
    )
    bias_part = jnp.sum(hidden_grad.astype(jnp.float32), axis=0) * grad_scale
    weight_grad, bias_grad = (
        lax.psum_scatter(weight_part, ("row", "col"), scatter_dimension=0, tiled=True),
        lax.psum_scatter(bias_part, ("row", "col"), scatter_dimension=0, tiled=True),
    )
    node_grad = aggregate(message_grad, tile_values, tile_index)
    return (activations, node_grad, weight_grad, bias_grad)


def solution(mesh):
    in_specs = (
        P(("row", "col"), None),
        P(),
        P(),
        P(("row", "col"), None),
        P(("row", "col"), None, None),
        P(("row", "col"), None),
    )
    out_specs = (
        P(("row", "col"), None),
        P(("row", "col"), None),
        P(("row", "col"), None),
        P(("row", "col")),
    )
    return jax.shard_map(local, mesh=mesh, in_specs=in_specs, out_specs=out_specs, check_vma=False)
```

profile of v0, /device:TPU:0, one launch (start us, length us, event | category | flops | bytes accessed | tf_op | source)
XLA Modules:
  0.0 466.7 jit_solution(152190468189280791)
XLA Ops:
  7.2 0.0 copy-start
  7.2 0.0 all-gather.3.cloned.1.call-start
  7.2 0.7 all-gather.3.cloned.1.call-update
  7.9 0.0 reduce-scatter.6.cloned.1.call-start
  8.0 2.3 all_gather.12
  10.3 0.8 compare_and_fusion.1
  11.1 0.0 copy-start.4
  11.1 2.7 gather_fusion
  13.8 0.0 copy-done.4
  13.8 8.6 %multiply_bitcast_fusion.3 = f32[32,256,256]{1,2,0:T(8,128)} fusion(f32[32]{0:T(128)S(1)} %bitcast_convert_fusion, bf16[32,256,256]{2,1,0:T(8,128)(2,1)} %param.14, bf16[32,256,256]{2,1,0:T(8,128)(2,1)} %gather_fusion, pred[32]{0:T(512)(128)(4,1)S(1)} %get-tuple-element.8), kind=kOutput, calls=%fused_computation.11 | convolution fusion | flops 1077936128 | bytes 16777376 | tf_op jit(solution)/shard_map/tnm,tmf->tnf/dot_general | solution.py:29
  22.5 9.0 %copy.23 = f32[32,256,256]{2,1,0:T(8,128)} copy(f32[32,256,256]{1,2,0:T(8,128)} %multiply_bitcast_fusion.3) | data formatting | bytes 16777216 | tf_op jit(solution)/shard_map/mul | solution.py:39
  31.4 2.4 broadcast.111.clone
  33.9 18.1 %scatter_fusion = f32[16,256,256]{2,1,0:T(8,128)} fusion(f32[16,256,256]{2,1,0:T(8,128)} %broadcast.111.clone, s32[32]{0:T(128)S(1)} %get-tuple-element.15, f32[32,256,256]{2,1,0:T(8,128)} %copy.23), kind=kCustom, calls=%fused_computation.4 | custom fusion | flops 2097152 | bytes 25165952 | tf_op jit(solution)/shard_map/scatter-add | solution.py:39
  52.0 3.7 convert_element_type.66
  55.7 0.0 reduce-scatter.6.cloned.1.call-update
  55.7 0.0 reduce-scatter.8.cloned.1.call-start
  55.8 18.1 %all-gather.3.cloned.1.call-done = bf16[4096,256]{1,0:T(8,128)(2,1)} async-done(((bf16[256,256]{1,0:T(8,128)(2,1)}), bf16[4096,256]{1,0:T(8,128)(2,1)}) %all-gather.3.cloned.1.call-update) | async-done | bytes 2097168 | tf_op jit(solution)/shard_map/all_gather | solution.py:15
  73.9 4.4 gather_fusion.1
  78.3 8.7 %multiply_bitcast_fusion.2 = f32[32,256,256]{1,2,0:T(8,128)} fusion(f32[32]{0:T(128)S(1)} %bitcast_convert_fusion, bf16[32,256,256]{2,1,0:T(8,128)(2,1)} %param.14, bf16[32,256,256]{2,1,0:T(8,128)(2,1)} %gather_fusion.1, pred[32]{0:T(512)(128)(4,1)S(1)} %get-tuple-element.13), kind=kOutput, calls=%fused_computation.10 | convolution fusion | flops 1077936128 | bytes 16777376 | tf_op jit(solution)/shard_map/tmn,tmf->tnf/dot_general | solution.py:32
  87.0 8.9 %copy.25 = f32[32,256,256]{2,1,0:T(8,128)} copy(f32[32,256,256]{1,2,0:T(8,128)} %multiply_bitcast_fusion.2) | data formatting | bytes 16777216 | tf_op jit(solution)/shard_map/mul | solution.py:44
  96.0 0.0 copy-start.5
  96.0 0.0 copy-start.6
  96.0 11.6 %scatter_fusion.1 = f32[2,256,256]{2,1,0:T(8,128)S(1)} fusion(f32[2,256,256]{2,1,0:T(8,128)S(1)} %broadcast.114.clone, s32[32]{0:T(128)S(1)} %get-tuple-element.16, f32[32,256,256]{2,1,0:T(8,128)} %copy.25), kind=kCustom, calls=%fused_computation.5 | custom fusion | flops 2097152 | bytes 25165952 | tf_op jit(solution)/shard_map/scatter-add | solution.py:44
  107.6 0.7 convert_element_type.69
  108.3 0.0 reduce-scatter.8.cloned.1.call-update
  108.3 0.0 all-gather.5.cloned.1.call-start
  108.4 48.0 %reduce-scatter.6.cloned.1.call-done = bf16[256,256]{1,0:T(8,128)(2,1)} async-done(((bf16[4096,256]{1,0:T(8,128)(2,1)}), bf16[256,256]{1,0:T(8,128)(2,1)}) %reduce-scatter.6.cloned.1.call-update) | async-done | bytes 131088 | tf_op jit(solution)/shard_map/reduce_scatter | solution.py:48
  156.4 6.8 %reduce-scatter.8.cloned.1.call-done = bf16[256,256]{1,0:T(8,128)(2,1)} async-done(((bf16[512,256]{1,0:T(8,128)(2,1)}), bf16[256,256]{1,0:T(8,128)(2,1)}) %reduce-scatter.8.cloned.1.call-update) | async-done | bytes 131088 | tf_op jit(solution)/shard_map/reduce_scatter | solution.py:51
  163.2 0.0 copy-done
  163.2 0.0 copy-done.5
  163.2 0.0 copy-done.6
  163.2 1.9 convert_reduce_fusion
  165.1 0.9 convolution_convert_fusion
  166.0 0.0 all-gather.5.cloned.1.call-update
  166.0 0.0 reduce-scatter.10.cloned.1.call-start
  166.1 2.4 all_gather.14
  168.4 2.7 gather_fusion.2
  171.2 8.6 %multiply_bitcast_fusion.1 = f32[32,256,256]{1,2,0:T(8,128)} fusion(f32[32]{0:T(128)S(1)} %bitcast_convert_fusion, bf16[32,256,256]{2,1,0:T(8,128)(2,1)} %param.14, bf16[32,256,256]{2,1,0:T(8,128)(2,1)} %gather_fusion.2, pred[32]{0:T(512)(128)(4,1)S(1)} %get-tuple-element.8), kind=kOutput, calls=%fused_computation.9 | convolution fusion | flops 1077936128 | bytes 16777376 | tf_op jit(solution)/shard_map/tnm,tmf->tnf/dot_general | solution.py:29
  179.8 9.0 %copy.27 = f32[32,256,256]{2,1,0:T(8,128)} copy(f32[32,256,256]{1,2,0:T(8,128)} %multiply_bitcast_fusion.1) | data formatting | bytes 16777216 | tf_op jit(solution)/shard_map/mul | solution.py:39
  188.8 2.4 broadcast.111
  191.2 18.2 %scatter_fusion.2 = f32[16,256,256]{2,1,0:T(8,128)} fusion(f32[16,256,256]{2,1,0:T(8,128)} %broadcast.111, s32[32]{0:T(128)S(1)} %get-tuple-element.15, f32[32,256,256]{2,1,0:T(8,128)} %copy.27), kind=kCustom, calls=%fused_computation.6 | custom fusion | flops 2097152 | bytes 25165952 | tf_op jit(solution)/shard_map/scatter-add | solution.py:39
  209.4 4.1 convert_element_type.77
  213.5 0.0 reduce-scatter.10.cloned.1.call-update
  213.5 0.0 reduce-scatter.12.cloned.1.call-start
  213.6 14.3 %all-gather.5.cloned.1.call-done = bf16[4096,256]{1,0:T(8,128)(2,1)} async-done(((bf16[256,256]{1,0:T(8,128)(2,1)}), bf16[4096,256]{1,0:T(8,128)(2,1)}) %all-gather.5.cloned.1.call-update) | async-done | bytes 2097168 | tf_op jit(solution)/shard_map/all_gather | solution.py:15
  227.9 4.4 gather_fusion.3
  232.3 8.7 %multiply_bitcast_fusion = f32[32,256,256]{1,2,0:T(8,128)} fusion(f32[32]{0:T(128)S(1)} %bitcast_convert_fusion, bf16[32,256,256]{2,1,0:T(8,128)(2,1)} %param.14, bf16[32,256,256]{2,1,0:T(8,128)(2,1)} %gather_fusion.3, pred[32]{0:T(512)(128)(4,1)S(1)} %get-tuple-element.13), kind=kOutput, calls=%fused_computation.8 | convolution fusion | flops 1077936128 | bytes 16777376 | tf_op jit(solution)/shard_map/tmn,tmf->tnf/dot_general | solution.py:32
  241.0 8.9 %copy.29 = f32[32,256,256]{2,1,0:T(8,128)} copy(f32[32,256,256]{1,2,0:T(8,128)} %multiply_bitcast_fusion) | data formatting | bytes 16777216 | tf_op jit(solution)/shard_map/mul | solution.py:44
  250.0 0.0 copy-start.2
  250.0 0.0 copy-start.3
  250.0 0.0 copy-start.1
  250.0 11.6 %scatter_fusion.3 = f32[2,256,256]{2,1,0:T(8,128)S(1)} fusion(f32[2,256,256]{2,1,0:T(8,128)S(1)} %broadcast.114, s32[32]{0:T(128)S(1)} %get-tuple-element.16, f32[32,256,256]{2,1,0:T(8,128)} %copy.29), kind=kCustom, calls=%fused_computation.7 | custom fusion | flops 2097152 | bytes 25165952 | tf_op jit(solution)/shard_map/scatter-add | solution.py:44
  261.6 0.7 convert_element_type.80
  262.3 0.0 reduce-scatter.12.cloned.1.call-update
  262.3 0.0 reduce-scatter.14.cloned.1.call-start
  262.4 0.9 convolution_multiply_fusion
  263.3 0.0 reduce-scatter.14.cloned.1.call-update
  263.4 39.7 %all-reduce = f32[256]{0:T(256)S(1)} all-reduce(f32[256]{0:T(256)S(1)} %broadcast_multiply_fusion), channel_id=7, replica_groups=mesh['row'=2,'col'=16] {'row','col'}, use_global_device_ids=true, to_apply=%region_10.13.clone | all-reduce | flops 256 | bytes 2048
  303.1 0.6 dynamic-slice
  303.7 6.9 %reduce-scatter.10.cloned.1.call-done = bf16[256,256]{1,0:T(8,128)(2,1)} async-done(((bf16[4096,256]{1,0:T(8,128)(2,1)}), bf16[256,256]{1,0:T(8,128)(2,1)}) %reduce-scatter.10.cloned.1.call-update) | async-done | bytes 131088 | tf_op jit(solution)/shard_map/reduce_scatter | solution.py:48
  310.5 6.4 %reduce-scatter.12.cloned.1.call-done = bf16[256,256]{1,0:T(8,128)(2,1)} async-done(((bf16[512,256]{1,0:T(8,128)(2,1)}), bf16[256,256]{1,0:T(8,128)(2,1)}) %reduce-scatter.12.cloned.1.call-update) | async-done | bytes 131088 | tf_op jit(solution)/shard_map/reduce_scatter | solution.py:51
  317.0 1.7 add_convert_fusion
  318.6 141.3 %reduce-scatter.14.cloned.1.call-done = f32[8,256]{1,0:T(8,128)} async-done(((f32[256,256]{1,0:T(8,128)}), f32[8,256]{1,0:T(8,128)}) %reduce-scatter.14.cloned.1.call-update) | async-done | bytes 8208 | tf_op jit(solution)/shard_map/reduce_scatter | solution.py:77
  459.9 0.0 copy-done.1
  (9 shorter events, 0.1 us)
Async XLA Ops:
  7.2 156.0 %copy-start = (bf16[256,256]{1,0:T(8,128)(2,1)S(1)}, bf16[256,256]{1,0:T(8,128)(2,1)}, u32[]{:S(2)}) copy-start(bf16[256,256]{1,0:T(8,128)(2,1)} %param.11) | copy-start | bytes 393220
  7.2 66.7 %all-gather.3.cloned.1.call-start = ((), (), s32[]{:S(2)}) async-start(), calls=%async_computation.6 | async-start | bytes 2228224 | tf_op jit(solution)/shard_map/all_gather | solution.py:15
  7.9 148.4 %reduce-scatter.6.cloned.1.call-start = ((), (), s32[]{:S(2)}) async-start(), calls=%async_computation.5 | async-start | bytes 2228224 | tf_op jit(solution)/shard_map/reduce_scatter | solution.py:48
  11.1 2.8 copy-start.4
  55.7 107.4 %reduce-scatter.8.cloned.1.call-start = ((), (), s32[]{:S(2)}) async-start(), calls=%async_computation.7 | async-start | bytes 393216 | tf_op jit(solution)/shard_map/reduce_scatter | solution.py:51
  96.0 67.2 %copy-start.5 = (bf16[256,256]{1,0:T(8,128)(2,1)S(1)}, bf16[256,256]{1,0:T(8,128)(2,1)}, u32[]{:S(2)}) copy-start(bf16[256,256]{1,0:T(8,128)(2,1)} %param.13) | copy-start | bytes 393220
  96.0 67.2 %copy-start.6 = (f32[256]{0:T(256)S(1)}, f32[256]{0:T(256)}, u32[]{:S(2)}) copy-start(f32[256]{0:T(256)} %param.12) | copy-start | bytes 3076
  108.3 119.6 %all-gather.5.cloned.1.call-start = ((), (), s32[]{:S(2)}) async-start(), calls=%async_computation.9 | async-start | bytes 2228224 | tf_op jit(solution)/shard_map/all_gather | solution.py:15
  166.0 144.5 %reduce-scatter.10.cloned.1.call-start = ((), (), s32[]{:S(2)}) async-start(), calls=%async_computation.8 | async-start | bytes 2228224 | tf_op jit(solution)/shard_map/reduce_scatter | solution.py:48
  213.5 103.4 %reduce-scatter.12.cloned.1.call-start = ((), (), s32[]{:S(2)}) async-start(), calls=%async_computation.10 | async-start | bytes 393216 | tf_op jit(solution)/shard_map/reduce_scatter | solution.py:51
  250.0 12.4 %copy-start.2 = (bf16[256,256]{1,0:T(8,128)(2,1)S(1)}, bf16[256,256]{1,0:T(8,128)(2,1)}, u32[]{:S(2)}) copy-start(bf16[256,256]{1,0:T(8,128)(2,1)} %reduce-scatter.6.cloned.1.call-done) | copy-start | bytes 393220
  250.0 12.4 %copy-start.3 = (bf16[256,256]{1,0:T(8,128)(2,1)S(1)}, bf16[256,256]{1,0:T(8,128)(2,1)}, u32[]{:S(2)}) copy-start(bf16[256,256]{1,0:T(8,128)(2,1)} %reduce-scatter.8.cloned.1.call-done) | copy-start | bytes 393220
  250.0 209.9 %copy-start.1 = (bf16[256,256]{1,0:T(8,128)(2,1)S(1)}, bf16[256,256]{1,0:T(8,128)(2,1)}, u32[]{:S(2)}) copy-start(bf16[256,256]{1,0:T(8,128)(2,1)} %param.11) | copy-start | bytes 393220
  262.3 197.5 %reduce-scatter.14.cloned.1.call-start = ((), (), s32[]{:S(2)}) async-start(), calls=%async_computation.11 | async-start | bytes 270336 | tf_op jit(solution)/shard_map/reduce_scatter | solution.py:77
Sparse Core Ops, SparseCore 0:
  10.8 63.0 all-gather.2
  76.2 80.1 reduce-scatter.5
  158.6 4.5 reduce-scatter.7
  166.4 61.4 all-gather.4
  230.0 80.4 reduce-scatter.9
  312.6 4.2 reduce-scatter.11
  319.8 140.0 reduce-scatter.13
where the time goes:
time: 468 us; the launch traced here: 467 us
  waiting for transfers between devices  243 us (52%)
  other arithmetic  71.2 us (15%)
  local copies, waits for them, and re-layouts  55.6 us (12%)
  blocking collectives  44.4 us (9%)
  matrix products  38.4 us (8%)
  between operations  14.3 us (3%)
    reduce_scatter x1, waiting for transfers between devices, local(): lax.psum_scatter(weight_part, ('row', 'col'), scatter_dimension=0, tiled=...  141 us
    reduce_scatter x2, waiting for transfers between devices, aggregate(): lax.psum_scatter(row_partial.astype(jnp.bfloat16), 'col', scatter_dimensi...  54.8 us
    unnamed x1, blocking collectives  39.7 us
    scatter-add x2, other arithmetic, aggregate(): row_partial = jnp.zeros((row_span, tile_size, feature_count), jnp.float32...  36.3 us
    all_gather x2, waiting for transfers between devices, aggregate(): row_group = lax.all_gather(node_data, 'col', axis=0, tiled=True)  32.4 us
    scatter-add x2, other arithmetic, aggregate(): column_partial = jnp.zeros((column_span, tile_size, feature_count), jnp.f...  23.1 us
    mul x2, local copies, waits for them, and re-layouts, aggregate(): forward_terms * live  17.9 us
    mul x2, local copies, waits for them, and re-layouts, aggregate(): mirror_terms * live  17.9 us
  transfers between devices with their start and end apart: 7, of which 7 were waited for; matrix products, arithmetic and copies ran while one was open for 35% of the time, Pallas kernels for 0%

commit v1 on v0

v1 whole, which is shorter than its diff:
```python
import functools

import jax
import jax.numpy as jnp
from jax import lax
from jax.experimental import pallas as pl
from jax.experimental.pallas import tpu as pltpu
from jax.sharding import PartitionSpec as P

MESH = pl.DeviceIdType.MESH
F32 = jnp.float32
BF16 = jnp.bfloat16
X, Y, LO, HI = 0, 1, 2, 3


def mm(a, b, ca, cb):
    return lax.dot_general(a, b, (((ca,), (cb,)), ((), ())), preferred_element_type=F32)


def pieces_of(tile):
    q = tile // 4
    return (
        (0, q, True, X, Y),
        (q, q, True, Y, X),
        (2 * q, 2 * q, False, X, Y),
    )


def kernel(
    n_row, n_col, scale,
    slot_ref, live_ref, feat_ref, w_ref, bias_ref, cot_ref, tiles_ref,
    act_ref, node_ref, wg_ref, bg_ref,
    G, S, R, V, M, MR, MS, TMP, WP, WX, WS, WR,
    ag_send, ag_recv, rs_send, rs_recv, v_send, v_recv, m_send, m_recv,
    wx_send, wx_recv, w_send, w_recv,
):
    tile = feat_ref.shape[0]
    nz = n_col // 4
    row = lax.axis_index("row")
    col = lax.axis_index("col")
    z = col // 4
    p = col % 4
    inner = row < n_row - 1
    pieces = pieces_of(tile)

    barrier = pltpu.get_barrier_semaphore()
    for j in range(1, n_row):
        pl.semaphore_signal(
            barrier, inc=1, device_id=(lax.rem(row + j, n_row), col), device_id_type=MESH
        )

    @pl.loop(1, n_col)
    def _(j):
        pl.semaphore_signal(
            barrier, inc=1, device_id=(row, lax.rem(col + j, n_col)), device_id_type=MESH
        )

    def flip(mask):
        return [lambda: p, lambda: p + 1 - 2 * (p % 2), lambda: p + 2 - 4 * (p // 2), lambda: 3 - p][mask]()

    bit = {X: 1, Y: 2}

    def place(mask, dz):
        return (z + dz) * 4 + flip(mask)

    def neighbour(direction):
        if direction in bit:
            return (row, place(bit[direction], 0))
        return (row, col - 4) if direction == LO else (row, col + 4)

    back = {X: X, Y: Y, LO: HI, HI: LO}

    def guarded(conds, fn):
        conds = [c for c in conds if c is not None]
        if not conds:
            fn()
        else:
            pl.when(functools.reduce(jnp.logical_and, conds))(fn)

    def aggregate(g):
        sends = []

        def gather_copy(q, src, direction):
            start, rows = pieces[q][:2]
            ref = G.at[g, src, pl.ds(start, rows)]
            return pltpu.make_async_remote_copy(
                src_ref=ref, dst_ref=ref, send_sem=ag_send.at[q, src, direction],
                recv_sem=ag_recv.at[g, q, src], device_id=neighbour(direction), device_id_type=MESH,
            )

        def gather_send(q, src, direction, conds):
            guarded(conds, lambda: gather_copy(q, src, direction).start())
            sends.append((conds, lambda: gather_copy(q, src, direction).wait_send()))

        def sum_copy(q, dst, direction):
            start, rows = pieces[q][:2]
            came = back[direction]
            return pltpu.make_async_remote_copy(
                src_ref=S.at[dst, pl.ds(start, rows)],
                dst_ref=R.at[g, came, dst, pl.ds(start, rows)],
                send_sem=rs_send.at[q, dst],
                recv_sem=rs_recv.at[g, q, came, dst],
                device_id=neighbour(direction), device_id_type=MESH,
            )

        def sum_wait(q, dst, came):
            start, rows = pieces[q][:2]
            pltpu.make_async_remote_copy(
                src_ref=S.at[dst, pl.ds(start, rows)],
                dst_ref=R.at[g, came, dst, pl.ds(start, rows)],
                send_sem=rs_send.at[q, dst],
                recv_sem=rs_recv.at[g, q, came, dst],
                device_id=neighbour(came), device_id_type=MESH,
            ).wait_recv()

        def sum_send(q, dst, direction, conds):
            guarded(conds, lambda: sum_copy(q, dst, direction).start())
            sends.append((conds, lambda: sum_copy(q, dst, direction).wait_send()))

        top, bottom = z < nz - 1, z > 0
        up_from = [(-d, [z >= d]) for d in range(1, nz)]
        down_from = [(d, [z + d < nz, inner]) for d in range(1, nz)]

        def row_copy(j):
            return pltpu.make_async_remote_copy(
                src_ref=V.at[g, row], dst_ref=V.at[g, row], send_sem=v_send.at[g, j],
                recv_sem=v_recv.at[g, row], device_id=(row - j, col), device_id_type=MESH,
            )

        for j in range(1, n_row):
            pl.when(row >= j)(lambda j=j: row_copy(j).start())
            sends.append(([row >= j], lambda j=j: row_copy(j).wait_send()))
        for q in range(len(pieces)):
            gather_send(q, col, X, [])
            gather_send(q, col, Y, [])
            gather_send(q, col, HI, [top])
            gather_send(q, col, LO, [bottom, inner])
        for k in range(n_row):
            @pl.when(k < row)
            def _(k=k):
                V[g, k] = jnp.zeros((tile, tile), BF16)

            @pl.when(k > row)
            def _(k=k):
                pltpu.make_async_remote_copy(
                    src_ref=V.at[g, k], dst_ref=V.at[g, k], send_sem=v_send.at[g, 0],
                    recv_sem=v_recv.at[g, k], device_id=(k, col), device_id_type=MESH,
                ).wait_recv()

        def load_tile(k, i):
            at = k * n_col + i
            live = jnp.full((tile, tile), live_ref[at], F32).astype(BF16)
            return tiles_ref[slot_ref[at]] * live

        @pl.loop(0, n_col)
        def _(i):
            total = mm(load_tile(0, i), V[g, 0], 1, 0)
            for k in range(1, n_row):
                total = total + mm(load_tile(k, i), V[g, k], 1, 0)
            S[i] = total.astype(BF16)

        events = []

        def add(t, conds, fn):
            events.append((t, len(events), conds, fn))

        def gather_event(t, q, mask, dz, conds, forward):
            def fn():
                src = place(mask, dz)
                start, rows = pieces[q][:2]
                ref = G.at[g, src, pl.ds(start, rows)]
                pltpu.make_async_remote_copy(
                    src_ref=ref, dst_ref=ref, send_sem=ag_send.at[q, src, X],
                    recv_sem=ag_recv.at[g, q, src], device_id=neighbour(X), device_id_type=MESH,
                ).wait_recv()
                for direction, more in forward:
                    guarded(more, lambda: gather_copy(q, src, direction).start())

            add(t, conds, fn)
            for direction, more in forward:
                sends.append((
                    conds + more,
                    lambda direction=direction: gather_copy(q, place(mask, dz), direction).wait_send(),
                ))

        def sum_event(t, q, mask, dz, conds, children, direction):
            start, rows = pieces[q][:2]

            def fn():
                dst = place(mask, dz)
                if children:
                    TMP[pl.ds(start, rows)] = S[dst, pl.ds(start, rows)].astype(F32)
                    for came, more in children:
                        def take(came=came):
                            sum_wait(q, dst, came)
                            TMP[pl.ds(start, rows)] += R[g, came, dst, pl.ds(start, rows)].astype(F32)

                        guarded(more, take)
                    if direction is not None:
                        S[dst, pl.ds(start, rows)] = TMP[pl.ds(start, rows)].astype(BF16)
                if direction is not None:
                    sum_copy(q, dst, direction).start()

            add(t, conds, fn)
            if direction is not None:
                sends.append((conds, lambda: sum_copy(q, place(mask, dz), direction).wait_send()))

        roots = []
        from_lo, from_hi = (LO, [bottom, inner]), (HI, [top])
        for q, (_, _, z_first, a, b) in enumerate(pieces):
            am, bm = bit[a], bit[b]
            every = [(0, [])] + up_from + down_from
            roots.append((q, [(a, []), (b, []), from_lo, from_hi]))
            if z_first:
                for dz, conds in up_from:
                    gather_event(-dz, q, 0, dz, conds, [(HI, [top]), (a, []), (b, [])])
                for dz, conds in down_from:
                    gather_event(dz, q, 0, dz, conds, [(LO, [bottom]), (a, []), (b, [])])
                for dz, conds in every:
                    d = abs(dz)
                    gather_event(d + 1.3, q, am, dz, conds, [(b, [])])
                    gather_event(100 + d, q, bm, dz, conds, [])
                    gather_event(101 + d, q, am | bm, dz, conds, [])
                    sum_event(-d * 0.01, q, bm, dz, conds, [], b)
                    sum_event(-d * 0.01, q, am | bm, dz, conds, [], b)
                    sum_event(2 + (nz - d) * 0.3, q, am, dz, conds, [(b, [])], a)
                for dz, conds in up_from:
                    sum_event(4 + nz + dz, q, 0, dz, conds, [(a, []), (b, []), (HI, [top])], LO)
                for dz, conds in down_from:
                    sum_event(4 + nz - dz, q, 0, dz, conds, [(a, []), (b, []), (LO, [bottom])], HI)
            else:
                spread = [(HI, [top]), (LO, [bottom, inner])]
                gather_event(1, q, am, 0, [], [(b, [])] + spread)
                gather_event(1.5, q, bm, 0, [], spread)
                gather_event(2.5, q, am | bm, 0, [], spread)
                for m in range(4):
                    for dz, conds in up_from:
                        gather_event(2.6 - dz, q, m, dz, conds, [(HI, [top])])
                        sum_event(0.8 * (nz - 1 + dz), q, m, dz, conds, [(HI, [top])], LO)
                    for dz, conds in down_from:
                        gather_event(2.6 + dz, q, m, dz, conds, [(LO, [bottom])])
                        sum_event(0.8 * (nz - 1 - dz), q, m, dz, conds, [(LO, [bottom])], HI)
                sum_event(nz + 1, q, am | bm, 0, [], [from_lo, from_hi], b)
                sum_event(nz + 1, q, bm, 0, [], [from_lo, from_hi], b)
                sum_event(nz + 2, q, am, 0, [], [(b, []), from_lo, from_hi], a)

        for _, _, conds, fn in sorted(events, key=lambda e: e[:2]):
            guarded(conds, fn)

        for k in range(n_row):
            M[k] = jnp.zeros((tile, tile), F32)

        @pl.loop(0, n_col)
        def _(i):
            @pl.when(jnp.logical_or(inner, i // 4 <= z))
            def _():
                block = G[g, i]
                for k in range(n_row):
                    @pl.when(k >= row)
                    def _(k=k):
                        M[k] += mm(block, load_tile(k, i), 1, 0)

        for k in range(n_row):
            MS[k] = M[k].astype(BF16)

        def mirror_copy(j):
            return pltpu.make_async_remote_copy(
                src_ref=MS.at[row + j], dst_ref=MR.at[g, row], send_sem=m_send.at[j],
                recv_sem=m_recv.at[g, row], device_id=(row + j, col), device_id_type=MESH,
            )

        for j in range(1, n_row):
            pl.when(row + j < n_row)(lambda j=j: mirror_copy(j).start())
            sends.append(([row + j < n_row], lambda j=j: mirror_copy(j).wait_send()))

        for q, children in roots:
            start, rows = pieces[q][:2]
            TMP[pl.ds(start, rows)] = S[col, pl.ds(start, rows)].astype(F32)
            for came, more in children:
                def take(came=came):
                    sum_wait(q, col, came)
                    TMP[pl.ds(start, rows)] += R[g, came, col, pl.ds(start, rows)].astype(F32)

                guarded(more, take)

        M[0] = MS[row].astype(F32)
        for k in range(n_row - 1):
            @pl.when(k < row)
            def _(k=k):
                pltpu.make_async_remote_copy(
                    src_ref=MS.at[k], dst_ref=MR.at[g, k], send_sem=m_send.at[0],
                    recv_sem=m_recv.at[g, k], device_id=(k, col), device_id_type=MESH,
                ).wait_recv()
                M[0] += MR[g, k].astype(F32)
        for conds, fn in sends:
            guarded(conds, fn)
        return (TMP[...] + M[0].T).astype(BF16)

    features = feat_ref[...]
    V[0, row] = features
    G[0, col] = features.astype(F32).T.astype(BF16)
    pl.semaphore_wait(barrier, n_row - 1 + n_col - 1)

    aggregated = aggregate(0)
    hidden = mm(aggregated, w_ref[...], 1, 0) + bias_ref[...]
    logistic = jax.nn.sigmoid(hidden)
    act_ref[...] = (hidden * logistic).astype(BF16)
    derivative = logistic * (1.0 + hidden * (1.0 - logistic))
    hidden_grad = (cot_ref[...].astype(F32) * derivative).astype(BF16)
    V[1, row] = mm(hidden_grad, w_ref[...], 1, 1).astype(BF16)
    G[1, col] = mm(w_ref[...], hidden_grad, 1, 1).astype(BF16)

    slice_rows = wg_ref.shape[0]
    weight_part = mm(aggregated, hidden_grad, 0, 0) * scale
    bias_part = jnp.sum(hidden_grad.astype(F32), axis=0, keepdims=True) * scale
    pad = jnp.zeros((WP.shape[2] - slice_rows - 1, tile), F32)
    for d in range(n_row * n_col):
        part = weight_part[d * slice_rows:(d + 1) * slice_rows]
        WP[d // n_col, d % n_col] = jnp.concatenate([part, bias_part, pad], axis=0).astype(BF16)

    def weight_row_copy(j):
        peer = lax.rem(row + j, n_row)
        return pltpu.make_async_remote_copy(
            src_ref=WP.at[peer], dst_ref=WX.at[j - 1], send_sem=wx_send.at[j - 1],
            recv_sem=wx_recv.at[j - 1], device_id=(peer, col), device_id_type=MESH,
        )

    for j in range(1, n_row):
        weight_row_copy(j).start()
    for j in range(1, n_row):
        weight_row_copy(j).wait()
    for i in range(n_col):
        total = WP[row, i].astype(F32)
        for j in range(1, n_row):
            total = total + WX[j - 1, i].astype(F32)
        WS[i] = total.astype(BF16)

    def weight_col_copy(j):
        peer = lax.rem(col + j, n_col)
        return pltpu.make_async_remote_copy(
            src_ref=WS.at[peer], dst_ref=WR.at[j - 1], send_sem=w_send.at[j - 1],
            recv_sem=w_recv.at[j - 1], device_id=(row, peer), device_id_type=MESH,
        )

    @pl.loop(1, n_col)
    def _(j):
        weight_col_copy(j).start()

    node_ref[...] = aggregate(1)

    @pl.loop(1, n_col)
    def _(j):
        weight_col_copy(j).wait()

    total = WS[col].astype(F32)
    for j in range(1, n_col):
        total = total + WR[j - 1].astype(F32)
    wg_ref[...] = total[:slice_rows]
    bg_ref[...] = total[slice_rows:slice_rows + 1]


def local(n_row, n_col, features, layer_weight, layer_bias, cotangent, tile_values, tile_index):
    tile, width = features.shape
    devices = n_row * n_col
    slice_rows = width // devices
    row = lax.axis_index("row")
    col = lax.axis_index("col")
    slots = tile_values.shape[0]
    first, second = tile_index[:, 0], tile_index[:, 1]
    where = jnp.where(first >= 0, second // n_col * n_col + first - row * n_col, -1)
    hit = where[None, :] == jnp.arange(devices, dtype=jnp.int32)[:, None]
    slot = jnp.sum(jnp.where(hit, jnp.arange(slots, dtype=jnp.int32)[None, :], 0), axis=1)
    live = jnp.sum(hit.astype(F32), axis=1)
    pad_rows = (slice_rows + 1 + 15) // 16 * 16
    n_piece = len(pieces_of(tile))
    dma = pltpu.SemaphoreType.DMA
    vmem = pl.BlockSpec(memory_space=pltpu.VMEM)
    smem = pl.BlockSpec(memory_space=pltpu.SMEM)
    activations, node_grad, weight_grad, bias_sum = pl.pallas_call(
        functools.partial(kernel, n_row, n_col, (tile * devices) ** -0.5),
        out_shape=(
            jax.ShapeDtypeStruct((tile, width), BF16),
            jax.ShapeDtypeStruct((tile, width), BF16),
            jax.ShapeDtypeStruct((slice_rows, width), F32),
            jax.ShapeDtypeStruct((1, width), F32),
        ),
        in_specs=[smem, smem] + [vmem] * 5,
        out_specs=(vmem,) * 4,
        scratch_shapes=[
            pltpu.VMEM((2, n_col, tile, width), BF16),
            pltpu.VMEM((n_col, tile, width), BF16),
            pltpu.VMEM((2, 4, n_col, tile, width), BF16),
            pltpu.VMEM((2, n_row, tile, width), BF16),
            pltpu.VMEM((n_row, tile, width), F32),
            pltpu.VMEM((2, n_row, tile, width), BF16),
            pltpu.VMEM((n_row, tile, width), BF16),
            pltpu.VMEM((tile, width), F32),
            pltpu.VMEM((n_row, n_col, pad_rows, width), BF16),
            pltpu.VMEM((n_row - 1, n_col, pad_rows, width), BF16),
            pltpu.VMEM((n_col, pad_rows, width), BF16),
            pltpu.VMEM((n_col - 1, pad_rows, width), BF16),
            dma((n_piece, n_col, 4)),
            dma((2, n_piece, n_col)),
            dma((n_piece, n_col)),
            dma((2, n_piece, 4, n_col)),
            dma((2, n_row)),
            dma((2, n_row)),
            dma((n_row,)),
            dma((2, n_row)),
            dma((n_row - 1,)),
            dma((n_row - 1,)),
            dma((n_col - 1,)),
            dma((n_col - 1,)),
        ],
        compiler_params=pltpu.CompilerParams(
            collective_id=0, has_side_effects=True, vmem_limit_bytes=67043328
        ),
        name="layer",
    )(slot, live, features, layer_weight, layer_bias[None, :], cotangent, tile_values)
    bias_rows = bias_sum.reshape(devices, slice_rows)
    bias_grad = lax.dynamic_index_in_dim(bias_rows, row * n_col + col, 0, keepdims=False)
    return activations, node_grad, weight_grad, bias_grad


def solution(mesh):
    n_row, n_col = mesh.shape["row"], mesh.shape["col"]
    split = P(("row", "col"), None)
    in_specs = (split, P(), P(), split, P(("row", "col"), None, None), split)
    out_specs = (split, split, split, P(("row", "col")))
    return jax.shard_map(
        functools.partial(local, n_row, n_col),
        mesh=mesh, in_specs=in_specs, out_specs=out_specs, check_vma=False,
    )
```

time: 468 us -> 115 us (0.25)
  the two profiles are of different devices: /device:TPU:0 before, /device:TPU:13 now
where the time goes in v1:
time: 115 us
  Pallas kernels  105 us (91%)
  local copies, waits for them, and re-layouts  5.55 us (5%)
  other arithmetic  3.36 us (3%)
    pallas_call x1, Pallas kernels, local(): pl.pallas_call(functools.partial(kernel, n_row, n_col, (tile * devices) *...  105 us
    unnamed x3, local copies, waits for them, and re-layouts  4.43 us

profile of v1, /device:TPU:13, one launch (start us, length us, event | category | flops | bytes accessed | tf_op | source)
XLA Modules:
  0.0 114.8 jit_solution(13660420604240965328)
XLA Ops:
  0.6 0.8 compare_select_fusion
  1.4 0.6 convert_reduce_fusion.live_ref
  2.0 0.6 select_reduce_fusion.slot_ref
  2.7 105.2 %layer.1 = (bf16[256,256]{1,0:T(8,128)(2,1)}, bf16[256,256]{1,0:T(8,128)(2,1)}, f32[8,256]{1,0:T(8,128)}, f32[1,256]{1,0:T(1,128)}) custom-call(s32[32]{0:T(128)} %select_reduce_fusion.slot_ref, f32[32]{0:T(128)} %convert_reduce_fusion.live_ref, bf16[256,256]{1,0:T(8,128)(2,1)} %feat_ref.1, bf16[256,256]{1,0:T(8,128)(2,1)} %w_ref.1, f32[1,256]{1,0:T(1,128)} %bitcast.20, ...), custom_call_target="tpu_custom_call" | custom-call | tf_op jit(solution)/shard_map/layer/pallas_call | solution.py:379
  107.9 0.5 broadcast.49
  108.4 1.3 %reduce.3 = f32[256]{0:T(256)S(1)} reduce(f32[1,256]{1,0:T(1,128)} %get-tuple-element.11, f32[]{:T(128)} %broadcast.49), dimensions={0}, to_apply=%get-tuple-element.11.reduce_sub_computation.3 | reduce | bytes 2052 | tf_op jit(solution)/shard_map/layer/pallas_call | solution.py:379
  109.8 0.1 reshape.51
  109.8 0.5 dynamic-slice_bitcast_fusion
  110.4 1.6 %copy.13 = bf16[256,256]{1,0:T(8,128)(2,1)} copy(bf16[256,256]{1,0:T(8,128)(2,1)} %get-tuple-element.16) | data formatting | bytes 262144
  111.9 1.6 %copy.14 = bf16[256,256]{1,0:T(8,128)(2,1)} copy(bf16[256,256]{1,0:T(8,128)(2,1)} %get-tuple-element.17) | data formatting | bytes 262144
  113.5 1.3 %copy.15 = f32[8,256]{1,0:T(8,128)} copy(f32[8,256]{1,0:T(8,128)} %get-tuple-element.18) | data formatting | bytes 16384

commit v2 on v1

--- a/solution.py
+++ b/solution.py
@@ -152,12 +152,14 @@
             live = jnp.full((tile, tile), live_ref[at], F32).astype(BF16)
             return tiles_ref[slot_ref[at]] * live
 
-        @pl.loop(0, n_col)
-        def _(i):
-            total = mm(load_tile(0, i), V[g, 0], 1, 0)
-            for k in range(1, n_row):
-                total = total + mm(load_tile(k, i), V[g, k], 1, 0)
-            S[i] = total.astype(BF16)
+        def forward_terms(y):
+            @pl.loop(0, 2 * nz)
+            def _(at):
+                i = at // 2 * 4 + 2 * y + at % 2
+                total = mm(load_tile(0, i), V[g, 0], 1, 0)
+                for k in range(1, n_row):
+                    total = total + mm(load_tile(k, i), V[g, k], 1, 0)
+                S[i] = total.astype(BF16)
 
         events = []
 
@@ -219,10 +221,11 @@
                 for dz, conds in every:
                     d = abs(dz)
                     gather_event(d + 1.3, q, am, dz, conds, [(b, [])])
-                    gather_event(100 + d, q, bm, dz, conds, [])
-                    gather_event(101 + d, q, am | bm, dz, conds, [])
-                    sum_event(-d * 0.01, q, bm, dz, conds, [], b)
-                    sum_event(-d * 0.01, q, am | bm, dz, conds, [], b)
+                    gather_event(100 + d if d else 3.8, q, bm, dz, conds, [])
+                    gather_event(100.1 + d if d else 3.85, q, am | bm, dz, conds, [])
+                    early = -1 if b == Y else 0
+                    sum_event(early - d * 0.01, q, bm, dz, conds, [], b)
+                    sum_event(early - d * 0.01, q, am | bm, dz, conds, [], b)
                     sum_event(2 + (nz - d) * 0.3, q, am, dz, conds, [(b, [])], a)
                 for dz, conds in up_from:
                     sum_event(4 + nz + dz, q, 0, dz, conds, [(a, []), (b, []), (HI, [top])], LO)
@@ -244,21 +247,25 @@
                 sum_event(nz + 1, q, bm, 0, [], [from_lo, from_hi], b)
                 sum_event(nz + 2, q, am, 0, [], [(b, []), from_lo, from_hi], a)
 
+        def mirror_terms(dz):
+            @pl.loop(0, 4 * n_row)
+            def _(at):
+                i = (z + dz) * 4 + at // n_row
+                k = at % n_row
+
+                @pl.when(k >= row)
+                def _():
+                    M[k] += mm(G[g, i], load_tile(k, i), 1, 0)
+
+        for dz, conds in [(0, [])] + up_from + down_from:
+            add(100.5 + abs(dz) if dz else 3.9, conds, lambda dz=dz: mirror_terms(dz))
+
+        for k in range(n_row):
+            M[k] = jnp.zeros((tile, tile), F32)
+        forward_terms(1 - p // 2)
+        add(-0.5, [], lambda: forward_terms(p // 2))
         for _, _, conds, fn in sorted(events, key=lambda e: e[:2]):
             guarded(conds, fn)
-
-        for k in range(n_row):
-            M[k] = jnp.zeros((tile, tile), F32)
-
-        @pl.loop(0, n_col)
-        def _(i):
-            @pl.when(jnp.logical_or(inner, i // 4 <= z))
-            def _():
-                block = G[g, i]
-                for k in range(n_row):
-                    @pl.when(k >= row)
-                    def _(k=k):
-                        M[k] += mm(block, load_tile(k, i), 1, 0)
 
         for k in range(n_row):
             MS[k] = M[k].astype(BF16)

time: 115 us -> 112 us (0.974)
  Pallas kernels: 105 us -> 102 us
    pallas_call x1, Pallas kernels: 105 us -> 102 us  [local(): pl.pallas_call(functools.partial(kernel, n_row, n_col, (tile * devices) *...]
where the time goes in v2:
time: 112 us
  Pallas kernels  102 us (91%)
  local copies, waits for them, and re-layouts  5.55 us (5%)
  other arithmetic  3.36 us (3%)
    pallas_call x1, Pallas kernels, local(): pl.pallas_call(functools.partial(kernel, n_row, n_col, (tile * devices) *...  102 us
    unnamed x3, local copies, waits for them, and re-layouts  4.43 us

profile of v2, /device:TPU:13, one launch (start us, length us, event | category | flops | bytes accessed | tf_op | source)
XLA Modules:
  0.0 111.9 jit_solution(2161499714126117124)
XLA Ops:
  0.6 0.8 compare_select_fusion
  1.4 0.6 convert_reduce_fusion.live_ref
  2.0 0.6 select_reduce_fusion.slot_ref
  2.7 102.3 %layer.1 = (bf16[256,256]{1,0:T(8,128)(2,1)}, bf16[256,256]{1,0:T(8,128)(2,1)}, f32[8,256]{1,0:T(8,128)}, f32[1,256]{1,0:T(1,128)}) custom-call(s32[32]{0:T(128)} %select_reduce_fusion.slot_ref, f32[32]{0:T(128)} %convert_reduce_fusion.live_ref, bf16[256,256]{1,0:T(8,128)(2,1)} %feat_ref.1, bf16[256,256]{1,0:T(8,128)(2,1)} %w_ref.1, f32[1,256]{1,0:T(1,128)} %bitcast.20, ...), custom_call_target="tpu_custom_call" | custom-call | tf_op jit(solution)/shard_map/layer/pallas_call | solution.py:386
  105.0 0.5 broadcast.49
  105.5 1.3 %reduce.3 = f32[256]{0:T(256)S(1)} reduce(f32[1,256]{1,0:T(1,128)} %get-tuple-element.11, f32[]{:T(128)} %broadcast.49), dimensions={0}, to_apply=%get-tuple-element.11.reduce_sub_computation.3 | reduce | bytes 2052 | tf_op jit(solution)/shard_map/layer/pallas_call | solution.py:386
  106.9 0.1 reshape.51
  106.9 0.5 dynamic-slice_bitcast_fusion
  107.5 1.6 %copy.13 = bf16[256,256]{1,0:T(8,128)(2,1)} copy(bf16[256,256]{1,0:T(8,128)(2,1)} %get-tuple-element.16) | data formatting | bytes 262144
  109.0 1.6 %copy.14 = bf16[256,256]{1,0:T(8,128)(2,1)} copy(bf16[256,256]{1,0:T(8,128)(2,1)} %get-tuple-element.17) | data formatting | bytes 262144
  110.6 1.3 %copy.15 = f32[8,256]{1,0:T(8,128)} copy(f32[8,256]{1,0:T(8,128)} %get-tuple-element.18) | data formatting | bytes 16384
